TPU v7x, 32 devices: a whole 2x2x4 slice. The times are simulated.
32 devices in a mesh: stn: 4 (over z), chan: 4 (over y, core), tile: 2 (over x).
Axes of the slice: x: 2, y: 2, z: 4, core: 2. Of those that a mesh axis runs over, the one named last changes fastest.
Arguments:
- model_image: bfloat16 [8, 64, 2048], P('tile', 'stn'), may hold values from -0.005859375 to 0.005859375
- station_beams: float32 [2, 64, 1024], replicated, may hold values from -6 to 6
- subgrid_offsets: int32 [4, 128, 2], P('chan'), may hold values from -4096 to 4064
- subgrid_stations: int32 [128, 2], P(('stn', 'tile')), may hold values from 0 to 63, as said below
- visibility_uv: float32 [2, 128, 512], P(None, ('stn', 'tile'), 'chan'), may hold values from 2 to 30
- observed: float32 [2, 32, 4, 512], P(None, ('stn', 'tile'), 'chan'), may hold values from -3 to 3
- live_counts: int32 [32, 4], P(('stn', 'tile'), 'chan'), may hold values from 1 to 8
Outputs:
- residual: float32 [2, 32, 4, 512], P(None, ('stn', 'tile'), 'chan')
Inputs may be any that keep to these rules, and one draw needn't show every extreme that they name: `subgrid_stations`: each row names two different stations. `live_counts`: rows with a time step at or beyond the count carry no data.
All inputs are finite; a program needn't handle non-finite values.
Results may differ from a plain program's by a relative error of at most 0.00071.
Values may be sent and summed in bfloat16 or wider, within the bound.
A program may use at most 64 MiB of HBM per device.

v0:
```python
import math
import jax
import jax.numpy as jnp
from jax import lax
from jax.sharding import PartitionSpec as P

SG = 32
NG = 8192
TIMES = 8
TILE_DEV = 4
TL = 64
SUB_TILE = 16
two_pi = 6.283185307179586


def phase_pair(products, modulus):
    angle_turns = jnp.mod(products, modulus).astype(jnp.float32) * (two_pi / modulus)
    return (jnp.cos(angle_turns), -jnp.sin(angle_turns))


def narrow_mix(pattern, left, right):
    return jnp.einsum(pattern, left, right, preferred_element_type=jnp.float32)


def exact_mix(pattern, left, right):
    return jnp.einsum(pattern, left, right, precision=lax.Precision.HIGHEST)


def tile_cuts(strip_rows, row_ids, offset_block, strip_half):
    block_size = offset_block.shape[0]
    columns = strip_rows.shape[1]
    pixel_idx = jnp.arange(SG, dtype=jnp.int32)
    col_pos = jnp.arange(columns, dtype=jnp.int32) - columns // 2
    v_index = offset_block[:, 1][:, None] + pixel_idx[None, :]
    ev_real, ev_imag = phase_pair(col_pos[:, None, None] * v_index[None, :, :], NG)
    phase_table = (
        jnp.stack([ev_real, ev_imag], axis=1)
        .reshape(columns, 2 * block_size * SG)
        .astype(jnp.bfloat16)
    )
    partial_q = jnp.dot(strip_rows, phase_table, preferred_element_type=jnp.float32).astype(
        jnp.bfloat16
    )
    partial_q = partial_q.reshape(strip_rows.shape[0], 2, block_size, SG)
    q_real = partial_q[:, 0]
    q_imag = partial_q[:, 1]
    u_index = offset_block[:, 0][:, None] + pixel_idx[None, :]
    row_pos = row_ids - strip_half
    eu_real, eu_imag = phase_pair(u_index[:, :, None] * row_pos[None, None, :], NG)
    eu_real = eu_real.astype(jnp.bfloat16)
    eu_imag = eu_imag.astype(jnp.bfloat16)
    cut_real = narrow_mix("jal,ljb->jab", eu_real, q_real) - narrow_mix(
        "jal,ljb->jab", eu_imag, q_imag
    )
    cut_imag = narrow_mix("jal,ljb->jab", eu_real, q_imag) + narrow_mix(
        "jal,ljb->jab", eu_imag, q_real
    )
    return jnp.stack([cut_real, cut_imag], axis=1).reshape(block_size, 2 * SG * SG)


def cuts_blocked(strip_rows, row_ids, offsets, strip_half):
    how_many = offsets.shape[0]
    block_size = math.gcd(how_many, 32)
    grouped = offsets.reshape(how_many // block_size, block_size, 2)
    stacked = lax.map(
        lambda offset_block: tile_cuts(strip_rows, row_ids, offset_block, strip_half), grouped
    )
    return stacked.reshape(how_many, 2 * SG * SG)


def predict(cut_rows, pair_ids, station_beams, uv_block):
    how_many = cut_rows.shape[0]
    cut_grid = cut_rows.reshape(how_many, 2, SG, SG)
    pixel_idx = jnp.arange(SG, dtype=jnp.int32)
    w_real, w_neg = phase_pair(pixel_idx[:, None] * pixel_idx[None, :], SG)
    w_imag = -w_neg
    c_real = cut_grid[:, 0]
    c_imag = cut_grid[:, 1]
    half_real = exact_mix("xa,jab->jxb", w_real, c_real) - exact_mix("xa,jab->jxb", w_imag, c_imag)
    half_imag = exact_mix("xa,jab->jxb", w_real, c_imag) + exact_mix("xa,jab->jxb", w_imag, c_real)
    sub_real = (
        exact_mix("jxb,yb->jxy", half_real, w_real) - exact_mix("jxb,yb->jxy", half_imag, w_imag)
    ) / (SG * SG)
    sub_imag = (
        exact_mix("jxb,yb->jxy", half_real, w_imag) + exact_mix("jxb,yb->jxy", half_imag, w_real)
    ) / (SG * SG)
    pixel_pos = pixel_idx.astype(jnp.float32)
    taper_line = 1.0 - ((2.0 * pixel_pos - (SG - 1)) / SG) ** 2
    taper_grid = (taper_line[:, None] * taper_line[None, :]).reshape(SG * SG)
    beam_first = station_beams[:, pair_ids[:, 0]]
    beam_second = station_beams[:, pair_ids[:, 1]]
    gain_real = (beam_first[0] * beam_second[0] + beam_first[1] * beam_second[1]) * taper_grid
    gain_imag = (beam_first[1] * beam_second[0] - beam_first[0] * beam_second[1]) * taper_grid
    flat_real = sub_real.reshape(how_many, SG * SG)
    flat_imag = sub_imag.reshape(how_many, SG * SG)
    weighted_real = (flat_real * gain_real - flat_imag * gain_imag).reshape(how_many, SG, SG)
    weighted_imag = (flat_real * gain_imag + flat_imag * gain_real).reshape(how_many, SG, SG)
    u_angle = uv_block[0][:, :, None] * pixel_pos[None, None, :] * (two_pi / SG)
    v_angle = uv_block[1][:, :, None] * pixel_pos[None, None, :] * (two_pi / SG)
    eu_real = jnp.cos(u_angle)
    eu_imag = -jnp.sin(u_angle)
    ev_real = jnp.cos(v_angle)
    ev_imag = -jnp.sin(v_angle)
    inner_real = exact_mix("jxy,jky->jxk", weighted_real, ev_real) - exact_mix(
        "jxy,jky->jxk", weighted_imag, ev_imag
    )
    inner_imag = exact_mix("jxy,jky->jxk", weighted_real, ev_imag) + exact_mix(
        "jxy,jky->jxk", weighted_imag, ev_real
    )
    vis_real = exact_mix("jkx,jxk->jk", eu_real, inner_real) - exact_mix(
        "jkx,jxk->jk", eu_imag, inner_imag
    )
    vis_imag = exact_mix("jkx,jxk->jk", eu_real, inner_imag) + exact_mix(
        "jkx,jxk->jk", eu_imag, inner_real
    )
    return jnp.stack([vis_real, vis_imag], axis=0)


def on_device(
    model_image,
    station_beams,
    subgrid_offsets,
    subgrid_stations,
    visibility_uv,
    observed,
    live_counts,
):
    tile_count = lax.axis_size("tile")
    columns = model_image.shape[2]
    strip_half = TILE_DEV * tile_count * TL // 2
    group_offsets = subgrid_offsets[0]
    stn_index = lax.axis_index("stn")
    tile_first = lax.axis_index("tile") * TILE_DEV
    tile_ids = jnp.arange(TILE_DEV, dtype=jnp.int32)
    group_size = SUB_TILE * tile_count
    station_offsets = lax.dynamic_slice_in_dim(group_offsets, stn_index * group_size, group_size, 0)
    shard_piece = lax.all_gather(model_image, "stn", axis=1, tiled=True)
    piece_rows = shard_piece.shape[1]
    piece_ids = (
        (tile_first + tile_ids)[:, None] * TL + jnp.arange(piece_rows, dtype=jnp.int32)[None, :]
    ).reshape(-1)
    piece_strip = shard_piece.reshape(TILE_DEV * piece_rows, columns)
    group_cuts = cuts_blocked(piece_strip, piece_ids, station_offsets, strip_half)
    own_cuts = lax.psum_scatter(group_cuts, "tile", scatter_dimension=0, tiled=True)
    predicted = predict(own_cuts, subgrid_stations, station_beams, visibility_uv)
    chan_count = lax.axis_size("chan")
    outgoing = predicted.reshape(2, SUB_TILE // chan_count, chan_count, predicted.shape[2])
    regrouped = lax.all_to_all(outgoing, "chan", split_axis=2, concat_axis=3, tiled=True)
    total_rows = regrouped.shape[3]
    time_step = jnp.mod(jnp.arange(total_rows, dtype=jnp.int32), TIMES)
    live_mask = time_step[None, None, :] < live_counts[:, :, None]
    return jnp.where(live_mask[None], observed - regrouped, 0.0)


def solution(mesh):
    return jax.shard_map(
        on_device,
        mesh=mesh,
        in_specs=(
            P("tile", "stn", None),
            P(),
            P("chan", None, None),
            P(("stn", "tile"), None),
            P(None, ("stn", "tile"), "chan"),
            P(None, ("stn", "tile"), "chan", None),
            P(("stn", "tile"), "chan"),
        ),
        out_specs=P(None, ("stn", "tile"), "chan", None),
        check_vma=False,
    )
```

profile of v0, /device:TPU:0, one launch (start us, length us, event | category | flops | bytes accessed | tf_op | source)
XLA Modules:
  0.0 118.8 jit_solution(3581766435553474679)
XLA Ops:
  6.5 0.0 copy-start
  6.5 0.0 all-gather.2.cloned.1.call-start
  6.5 0.7 all-gather.2.cloned.1.call-update
  7.3 0.0 reduce-scatter.2.cloned.1.call-start
  7.3 0.8 dynamic-slice_bitcast_fusion
  8.1 0.1 iota_add_fusion
  8.2 0.1 iota_add_fusion.1
  8.2 0.1 add_add_fusion
  8.3 0.8 fusion.66
  9.1 0.0 copy-done
  9.1 0.7 gather_fusion
  9.9 0.7 gather_fusion.1
  10.6 0.1 sub.67
  10.7 0.1 add.237
  10.8 0.1 sub.77
  11.0 35.5 %cosine_convert_fusion = (bf16[2048,1,32,32]{0,3,2,1:T(8,128)(2,1)S(1)}, bf16[2048,1,32,32]{0,3,2,1:T(8,128)(2,1)}) fusion(s32[32,32]{1,0:T(8,128)S(1)} %iota_add_fusion, s32[2048]{0:T(1024)S(1)} %iota_add_fusion.2), kind=kLoop, calls=%fused_computation.12 | loop fusion | flops 35651584 | bytes 8400896 | tf_op jit(solution)/shard_map/convert
  46.4 6.2 %pad_maximum_fusion = bf16[2048,2,32,32]{0,3,2,1:T(8,128)(2,1)} fusion(bf16[2048,1,32,32]{0,3,2,1:T(8,128)(2,1)} %get-tuple-element.31, bf16[2048,1,32,32]{0,3,2,1:T(8,128)(2,1)S(1)} %get-tuple-element.30), kind=kLoop, calls=%fused_computation.10 | loop fusion | flops 4194304 | bytes 16777216 | tf_op jit(solution)/shard_map/while/body/eval_jaxpr/stack | solution.py:37
  52.6 0.0 all-gather.2.cloned.1.call-done
  52.6 6.0 %convolution_convert_fusion = bf16[2048,256]{1,0:T(8,128)(2,1)S(1)} fusion(bf16[2048,2048]{0,1:T(8,128)(2,1)} %bitcast.90, bf16[256,2048]{1,0:T(8,128)(2,1)} %bitcast.96), kind=kOutput, calls=%fused_computation.13 | convolution fusion | flops 2148007936 | bytes 10485760 | tf_op jit(solution)/shard_map/while/body/eval_jaxpr/dot_general | solution.py:41
  58.6 4.0 %fusion.15 = f32[32,32,32]{2,1,0:T(8,128)S(1)} fusion(s32[256]{0:T(256)S(1)} %sub.67, s32[32,32]{1,0:T(8,128)S(1)} %iota_add_fusion.1, bf16[256,2,32,32]{0,3,2,1:T(8,128)(2,1)S(1)} %bitcast.97), kind=kOutput, calls=%fused_computation.44 | convolution fusion | flops 20709376 | bytes 672768 | tf_op jit(solution)/shard_map/while/body/eval_jaxpr/jal,ljb->jab/dot_general | solution.py:22
  62.6 4.0 %fusion.14 = f32[32,32,32]{2,1,0:T(8,128)S(1)} fusion(s32[256]{0:T(256)S(1)} %sub.67, s32[32,32]{1,0:T(8,128)S(1)} %iota_add_fusion.1, bf16[256,2,32,32]{0,3,2,1:T(8,128)(2,1)S(1)} %bitcast.98), kind=kOutput, calls=%fused_computation.43 | convolution fusion | flops 20709376 | bytes 672768 | tf_op jit(solution)/shard_map/while/body/eval_jaxpr/jal,ljb->jab/dot_general | solution.py:22
  66.6 0.0 copy-start.2
  66.6 4.3 %fusion.4 = f32[32,1,32,32]{3,2,0,1:T(8,128)S(1)} fusion(f32[32,32,32]{2,1,0:T(8,128)S(1)} %fusion.15, s32[256]{0:T(256)S(1)} %sub.67, s32[32,32]{1,0:T(8,128)S(1)} %iota_add_fusion.1, bf16[256,2,32,32]{0,3,2,1:T(8,128)(2,1)S(1)} %bitcast.99), kind=kOutput, calls=%fused_computation.22 | convolution fusion | flops 21004288 | bytes 1197056 | tf_op jit(solution)/shard_map/while/body/eval_jaxpr/jal,ljb->jab/dot_general | solution.py:22
  70.9 4.1 %fusion.3 = f32[32,1,32,32]{3,2,0,1:T(8,128)S(1)} fusion(f32[32,32,32]{2,1,0:T(8,128)S(1)} %fusion.14, s32[256]{0:T(256)S(1)} %sub.67, s32[32,32]{1,0:T(8,128)S(1)} %iota_add_fusion.1, bf16[256,2,32,32]{0,3,2,1:T(8,128)(2,1)S(1)} %bitcast.100), kind=kOutput, calls=%fused_computation.20 | convolution fusion | flops 21004288 | bytes 1197056 | tf_op jit(solution)/shard_map/while/body/eval_jaxpr/jal,ljb->jab/dot_general | solution.py:22
  75.0 0.0 copy-start.3
  75.0 0.0 copy-start.1
  75.0 0.1 pad_maximum_fusion.1
  75.1 0.1 copy.26
  75.2 1.2 %reshape.278 = f32[32,2048]{1,0:T(8,128)} reshape(f32[32,2,32,32]{3,2,1,0:T(8,128)S(1)} %copy.26) | data formatting | bytes 524288 | tf_op jit(solution)/shard_map/reshape | solution.py:68
  76.4 0.0 reduce-scatter.2.cloned.1.call-update
  76.4 0.1 broadcast_multiply_fusion
  76.5 0.0 copy-done.2
  76.5 14.6 %reduce-scatter.2.cloned.1.call-done = f32[16,2048]{1,0:T(8,128)} async-done(((f32[32,2048]{1,0:T(8,128)}), f32[16,2048]{1,0:T(8,128)}) %reduce-scatter.2.cloned.1.call-update) | async-done | bytes 131088 | tf_op jit(solution)/shard_map/reduce_scatter | solution.py:144
  91.1 1.1 reshape.279
  92.2 0.6 fusion.23
  92.8 0.6 fusion.22
  93.4 0.6 fusion.10
  94.0 0.6 fusion.46
  94.6 0.6 fusion.39
  95.2 0.6 fusion.9
  95.8 0.9 fusion.8
  96.6 0.6 multiply_add_fusion
  97.2 1.3 %fusion.18 = f32[16,32,128]{2,1,0:T(8,128)S(1)} fusion(f32[16,32,32]{2,1,0:T(8,128)S(1)} %get-tuple-element.27, f32[16,128]{1,0:T(8,128)S(1)} %get-tuple-element.33, f32[32]{0:T(128)S(1)} %iota_convert_fusion), kind=kOutput, calls=%fused_computation.56 | convolution fusion | flops 25296896 | bytes 336000 | tf_op jit(solution)/shard_map/jxy,jky->jxk/dot_general | solution.py:26
  98.6 1.3 %fusion.20 = f32[16,32,128]{2,1,0:T(8,128)S(1)} fusion(f32[16,32,32]{2,1,0:T(8,128)S(1)} %get-tuple-element.27, f32[16,128]{1,0:T(8,128)S(1)} %get-tuple-element.33, f32[32]{0:T(128)S(1)} %iota_convert_fusion), kind=kOutput, calls=%fused_computation.57 | convolution fusion | flops 25362432 | bytes 336000 | tf_op jit(solution)/shard_map/jxy,jky->jxk/dot_general | solution.py:26
  99.9 1.3 %fusion.6 = f32[16,128,32]{1,2,0:T(8,128)S(1)} fusion(f32[16,32,128]{2,1,0:T(8,128)S(1)} %fusion.18, f32[16,32,32]{2,1,0:T(8,128)S(1)} %get-tuple-element.26, f32[16,128]{1,0:T(8,128)S(1)} %get-tuple-element.33, f32[32]{0:T(128)S(1)} %iota_convert_fusion), kind=kOutput, calls=%fused_computation.26 | convolution fusion | flops 25427968 | bytes 598144 | tf_op jit(solution)/shard_map/jxy,jky->jxk/dot_general | solution.py:26
  101.2 2.4 %multiply_reduce_fusion.2 = (f32[16,128]{1,0:T(8,128)S(1)}, f32[16,128]{1,0:T(8,128)S(1)}, f32[16,128]{1,0:T(8,128)S(1)}, f32[16,128]{1,0:T(8,128)S(1)}) fusion(f32[32]{0:T(128)S(1)} %iota_convert_fusion, f32[16,128]{1,0:T(8,128)S(1)} %get-tuple-element.32, f32[16,128,32]{1,2,0:T(8,128)S(1)} %fusion.6, f32[16,32,128]{2,1,0:T(8,128)S(1)} %fusion.20, ...), kind=kOutput, calls=%fused_computation.49 | convolution fusion | flops 26075136 | bytes 639104 | tf_op jit(solution)/shard_map/jxy,jky->jxk/dot_general | solution.py:26
  103.6 0.6 copy.33
  104.2 3.3 %all-to-all-start = ((f32[2,4,4,128]{3,1,0,2:T(4,128)}), f32[2,4,4,128]{3,1,0,2:T(4,128)S(1)}, u32[]{:S(2)}, u32[]{:S(2)}) async-start(f32[2,4,4,128]{3,1,0,2:T(4,128)} %copy.33), calls=%async_computation.1 | async-start | bytes 32768 | tf_op jit(solution)/shard_map/all_to_all | solution.py:148
  107.5 0.0 copy-done.3
  107.5 0.1 broadcast_compare_fusion
  107.6 3.7 %all-to-all-done = f32[2,4,4,128]{3,1,0,2:T(4,128)S(1)} async-done(((f32[2,4,4,128]{3,1,0,2:T(4,128)}), f32[2,4,4,128]{3,1,0,2:T(4,128)S(1)}, u32[]{:S(2)}, u32[]{:S(2)}) %all-to-all-start) | async-done | bytes 16416 | tf_op jit(solution)/shard_map/all_to_all | solution.py:148
  111.3 0.0 copy-done.1
  111.4 0.6 copy.36
  (15 shorter events, 0.1 us)
Async XLA Ops:
  6.5 2.6 %copy-start = (f32[2,64,1024]{2,1,0:T(8,128)S(1)}, f32[2,64,1024]{2,1,0:T(8,128)}, u32[]{:S(2)}) copy-start(f32[2,64,1024]{2,1,0:T(8,128)} %param.8) | copy-start | bytes 1572868
  6.5 46.1 %all-gather.2.cloned.1.call-start = ((), (), s32[]{:S(2)}) async-start(), calls=%async_computation.2 | async-start | bytes 1310720 | tf_op jit(solution)/shard_map/all_gather | solution.py:137
  7.3 83.8 %reduce-scatter.2.cloned.1.call-start = ((), (), s32[]{:S(2)}) async-start(), calls=%async_computation.3 | async-start | bytes 393216 | tf_op jit(solution)/shard_map/reduce_scatter | solution.py:144
  66.6 9.9 %copy-start.2 = (f32[2,16,128]{2,1,0:T(8,128)S(1)}, f32[2,16,128]{2,1,0:T(8,128)}, u32[]{:S(2)}) copy-start(f32[2,16,128]{2,1,0:T(8,128)} %param.11) | copy-start | bytes 49156
  75.0 32.5 %copy-start.3 = (s32[4,1]{0,1:T(1,128)S(1)}, s32[4,1]{0,1:T(1,128)}, u32[]{:S(2)}) copy-start(s32[4,1]{0,1:T(1,128)} %param.13) | copy-start | bytes 52
  75.0 36.3 %copy-start.1 = (f32[2,4,1,512]{3,2,1,0:T(1,128)S(1)}, f32[2,4,1,512]{3,2,1,0:T(1,128)}, u32[]{:S(2)}) copy-start(f32[2,4,1,512]{3,2,1,0:T(1,128)} %param.12) | copy-start | bytes 49156
  104.2 7.1 %all-to-all-start = ((f32[2,4,4,128]{3,1,0,2:T(4,128)}), f32[2,4,4,128]{3,1,0,2:T(4,128)S(1)}, u32[]{:S(2)}, u32[]{:S(2)}) async-start(f32[2,4,4,128]{3,1,0,2:T(4,128)} %copy.33), calls=%async_computation.1 | async-start | bytes 32768 | tf_op jit(solution)/shard_map/all_to_all | solution.py:148
Sparse Core Ops, SparseCore 0:
  8.9 30.7 all-gather.1
  76.6 14.4 reduce-scatter.1
where the time goes:
time: 119 us
  other arithmetic  43 us (36%)
  matrix products  33.7 us (28%)
  waiting for transfers between devices  19 us (16%)
  between operations  13.6 us (11%)
  local copies, waits for them, and re-layouts  6.18 us (5%)
  starting transfers between devices  3.3 us (3%)
    another operation x1, other arithmetic  35.5 us
    dot_general x4, matrix products, narrow_mix(): return jnp.einsum(pattern, left, right, preferred_element_type=jnp.float32)  16.4 us
    reduce_scatter x1, waiting for transfers between devices, on_device(): lax.psum_scatter(group_cuts, 'tile', scatter_dimension=0, tiled=True)  14.6 us
    dot_general x12, matrix products, exact_mix(): return jnp.einsum(pattern, left, right, precision=lax.Precision.HIGHEST)  11.3 us
    another operation x1, other arithmetic, tile_cuts(): jnp.stack([ev_real, ev_imag], axis=1).reshape(columns, 2 * block_size * SG)  6.18 us
    dot_general x1, matrix products, tile_cuts(): jnp.dot(strip_rows, phase_table, preferred_element_type=jnp.float32)  6 us
    all_to_all x1, waiting for transfers between devices, on_device(): lax.all_to_all(outgoing, 'chan', split_axis=2, concat_axis=3, tiled=True)  3.74 us
    all_to_all x1, starting transfers between devices, on_device(): lax.all_to_all(outgoing, 'chan', split_axis=2, concat_axis=3, tiled=True)  3.25 us
  transfers between devices with their start and end apart: 3, of which 2 were waited for; matrix products, arithmetic and copies ran while one was open for 38% of the time, Pallas kernels for 0%

commit v1 on v0

--- a/solution.py
+++ b/solution.py
@@ -11,6 +11,29 @@
 TL = 64
 SUB_TILE = 16
 two_pi = 6.283185307179586
+
+
+def split_up(array, dim, size):
+    lengths = array.shape
+    parts = array.reshape(*lengths[:dim], size, lengths[dim] // size, *lengths[dim + 1 :])
+    return jnp.moveaxis(parts, dim, 0)
+
+
+def in_order(pieces, dim):
+    shape = list(pieces.shape[1:])
+    shape[dim] *= pieces.shape[0]
+    return jnp.moveaxis(pieces, 0, dim).reshape(shape)
+
+
+def exchange_in_pairs(x, axis, split_dim, concat_dim):
+    size, position = (lax.axis_size(axis), lax.axis_index(axis))
+    blocks = split_up(x, split_dim, size)
+    gathered = [blocks[position]]
+    for hop in range(1, size):
+        sent = blocks[position ^ hop]
+        gathered.append(lax.ppermute(sent, axis, [(i, i ^ hop) for i in range(size)]))
+    blocks = jnp.stack(gathered)[position ^ jnp.arange(size)]
+    return in_order(blocks, concat_dim)
 
 
 def phase_pair(products, modulus):
@@ -145,7 +168,7 @@
     predicted = predict(own_cuts, subgrid_stations, station_beams, visibility_uv)
     chan_count = lax.axis_size("chan")
     outgoing = predicted.reshape(2, SUB_TILE // chan_count, chan_count, predicted.shape[2])
-    regrouped = lax.all_to_all(outgoing, "chan", split_axis=2, concat_axis=3, tiled=True)
+    regrouped = exchange_in_pairs(outgoing, "chan", 2, 3)
     total_rows = regrouped.shape[3]
     time_step = jnp.mod(jnp.arange(total_rows, dtype=jnp.int32), TIMES)
     live_mask = time_step[None, None, :] < live_counts[:, :, None]

time: 119 us -> 117 us (0.983)
  starting transfers between devices: 3.3 us -> 1.96 us
  other arithmetic: 43 us -> 44.3 us
    all_to_all x1 -> x0, waiting for transfers between devices: 3.74 us -> none  [on_device(): lax.all_to_all(outgoing, 'chan', split_axis=2, concat_axis=3, tiled=True)]
    all_to_all x1 -> x0, starting transfers between devices: 3.25 us -> none  [on_device(): lax.all_to_all(outgoing, 'chan', split_axis=2, concat_axis=3, tiled=True)]
    ppermute x0 -> x3, waiting for transfers between devices: none -> 2.7 us  [exchange_in_pairs(): lax.ppermute(sent, axis, [(i, i ^ hop) for i in range(size)])]
    ppermute x0 -> x3, starting transfers between devices: none -> 1.92 us  [exchange_in_pairs(): lax.ppermute(sent, axis, [(i, i ^ hop) for i in range(size)])]
    another operation x1 -> x2, other arithmetic: 35.5 us -> 35.5 us
  transfers between devices with their start and end apart: 3 -> 5, of which waited for: 2 -> 3; matrix products, arithmetic and copies ran while one was open for 38% -> 39% of each run, Pallas kernels for 0% -> 0%
where the time goes in v1:
time: 117 us
  other arithmetic  44.3 us (38%)
  matrix products  33.7 us (29%)
  waiting for transfers between devices  18 us (15%)
  between operations  13.7 us (12%)
  local copies, waits for them, and re-layouts  5.5 us (5%)
  starting transfers between devices  1.96 us (2%)
    another operation x1, other arithmetic  35.5 us
    dot_general x4, matrix products, narrow_mix(): return jnp.einsum(pattern, left, right, preferred_element_type=jnp.float32)  16.4 us
    reduce_scatter x1, waiting for transfers between devices, on_device(): lax.psum_scatter(group_cuts, 'tile', scatter_dimension=0, tiled=True)  14.6 us
    dot_general x12, matrix products, exact_mix(): return jnp.einsum(pattern, left, right, precision=lax.Precision.HIGHEST)  11.4 us
    another operation x1, other arithmetic, tile_cuts(): jnp.stack([ev_real, ev_imag], axis=1).reshape(columns, 2 * block_size * SG)  6.18 us
    dot_general x1, matrix products, tile_cuts(): jnp.dot(strip_rows, phase_table, preferred_element_type=jnp.float32)  6 us
    ppermute x3, waiting for transfers between devices, exchange_in_pairs(): lax.ppermute(sent, axis, [(i, i ^ hop) for i in range(size)])  2.7 us
  transfers between devices with their start and end apart: 5, of which 3 were waited for; matrix products, arithmetic and copies ran while one was open for 39% of the time, Pallas kernels for 0%

profile of v1, /device:TPU:0, one launch (start us, length us, event | category | flops | bytes accessed | tf_op | source)
XLA Modules:
  0.0 117.1 jit_solution(6607002912501205430)
XLA Ops:
  6.5 0.0 copy-start
  6.5 0.0 all-gather.2.cloned.1.call-start
  6.5 0.7 all-gather.2.cloned.1.call-update
  7.3 0.0 reduce-scatter.2.cloned.1.call-start
  7.3 0.8 fusion.81
  8.1 0.1 iota_add_fusion
  8.2 0.1 iota_add_fusion.1
  8.3 0.1 add_add_fusion
  8.3 0.8 fusion.82
  9.1 0.0 copy-done
  9.1 0.7 gather_fusion
  9.9 0.7 gather_fusion.1
  10.6 0.7 broadcast_compare_fusion
  11.4 0.1 sub.67
  11.5 0.1 add.259
  11.6 0.1 sub.77
  11.7 35.5 %cosine_convert_fusion = (bf16[2048,1,32,32]{0,3,2,1:T(8,128)(2,1)S(1)}, bf16[2048,1,32,32]{0,3,2,1:T(8,128)(2,1)}) fusion(s32[32,32]{1,0:T(8,128)S(1)} %iota_add_fusion, s32[2048]{0:T(1024)S(1)} %iota_add_fusion.2), kind=kLoop, calls=%fused_computation.13 | loop fusion | flops 35651584 | bytes 8400896 | tf_op jit(solution)/shard_map/convert
  47.2 6.2 %pad_maximum_fusion = bf16[2048,2,32,32]{0,3,2,1:T(8,128)(2,1)} fusion(bf16[2048,1,32,32]{0,3,2,1:T(8,128)(2,1)} %get-tuple-element.31, bf16[2048,1,32,32]{0,3,2,1:T(8,128)(2,1)S(1)} %get-tuple-element.30), kind=kLoop, calls=%fused_computation.11 | loop fusion | flops 4194304 | bytes 16777216 | tf_op jit(solution)/shard_map/while/body/eval_jaxpr/stack | solution.py:60
  53.3 0.0 all-gather.2.cloned.1.call-done
  53.4 6.0 %convolution_convert_fusion = bf16[2048,256]{1,0:T(8,128)(2,1)S(1)} fusion(bf16[2048,2048]{0,1:T(8,128)(2,1)} %bitcast.105, bf16[256,2048]{1,0:T(8,128)(2,1)} %bitcast.120), kind=kOutput, calls=%fused_computation.14 | convolution fusion | flops 2148007936 | bytes 10485760 | tf_op jit(solution)/shard_map/while/body/eval_jaxpr/dot_general | solution.py:64
  59.4 4.0 %fusion.15 = f32[32,32,32]{2,1,0:T(8,128)S(1)} fusion(s32[256]{0:T(256)S(1)} %sub.67, s32[32,32]{1,0:T(8,128)S(1)} %iota_add_fusion.1, bf16[256,2,32,32]{0,3,2,1:T(8,128)(2,1)S(1)} %bitcast.121), kind=kOutput, calls=%fused_computation.45 | convolution fusion | flops 20709376 | bytes 672768 | tf_op jit(solution)/shard_map/while/body/eval_jaxpr/jal,ljb->jab/dot_general | solution.py:45
  63.4 4.0 %fusion.14 = f32[32,32,32]{2,1,0:T(8,128)S(1)} fusion(s32[256]{0:T(256)S(1)} %sub.67, s32[32,32]{1,0:T(8,128)S(1)} %iota_add_fusion.1, bf16[256,2,32,32]{0,3,2,1:T(8,128)(2,1)S(1)} %bitcast.122), kind=kOutput, calls=%fused_computation.44 | convolution fusion | flops 20709376 | bytes 672768 | tf_op jit(solution)/shard_map/while/body/eval_jaxpr/jal,ljb->jab/dot_general | solution.py:45
  67.4 0.0 copy-start.2
  67.4 4.3 %fusion.4 = f32[32,1,32,32]{3,2,0,1:T(8,128)S(1)} fusion(f32[32,32,32]{2,1,0:T(8,128)S(1)} %fusion.15, s32[256]{0:T(256)S(1)} %sub.67, s32[32,32]{1,0:T(8,128)S(1)} %iota_add_fusion.1, bf16[256,2,32,32]{0,3,2,1:T(8,128)(2,1)S(1)} %bitcast.123), kind=kOutput, calls=%fused_computation.23 | convolution fusion | flops 21004288 | bytes 1197056 | tf_op jit(solution)/shard_map/while/body/eval_jaxpr/jal,ljb->jab/dot_general | solution.py:45
  71.7 4.1 %fusion.3 = f32[32,1,32,32]{3,2,0,1:T(8,128)S(1)} fusion(f32[32,32,32]{2,1,0:T(8,128)S(1)} %fusion.14, s32[256]{0:T(256)S(1)} %sub.67, s32[32,32]{1,0:T(8,128)S(1)} %iota_add_fusion.1, bf16[256,2,32,32]{0,3,2,1:T(8,128)(2,1)S(1)} %bitcast.124), kind=kOutput, calls=%fused_computation.21 | convolution fusion | flops 21004288 | bytes 1197056 | tf_op jit(solution)/shard_map/while/body/eval_jaxpr/jal,ljb->jab/dot_general | solution.py:45
  75.8 0.0 copy-start.1
  75.8 0.1 pad_maximum_fusion.1
  75.9 0.1 copy.19
  76.0 1.2 %reshape.300 = f32[32,2048]{1,0:T(8,128)} reshape(f32[32,2,32,32]{3,2,1,0:T(8,128)S(1)} %copy.19) | data formatting | bytes 524288 | tf_op jit(solution)/shard_map/reshape | solution.py:91
  77.2 0.0 reduce-scatter.2.cloned.1.call-update
  77.2 0.1 broadcast_multiply_fusion
  77.3 0.0 copy-done.2
  77.3 14.6 %reduce-scatter.2.cloned.1.call-done = f32[16,2048]{1,0:T(8,128)} async-done(((f32[32,2048]{1,0:T(8,128)}), f32[16,2048]{1,0:T(8,128)}) %reduce-scatter.2.cloned.1.call-update) | async-done | bytes 131088 | tf_op jit(solution)/shard_map/reduce_scatter | solution.py:167
  91.8 1.1 reshape.301
  92.9 0.6 fusion.23
  93.5 0.6 fusion.22
  94.1 0.6 fusion.10
  94.7 0.6 fusion.46
  95.3 0.6 fusion.39
  95.9 0.6 fusion.9
  96.5 0.9 fusion.8
  97.4 0.6 multiply_add_fusion
  98.0 1.3 %fusion.20 = f32[16,32,128]{2,1,0:T(8,128)S(1)} fusion(f32[16,32,32]{2,1,0:T(8,128)S(1)} %get-tuple-element.27, f32[16,128]{1,0:T(8,128)S(1)} %get-tuple-element.37, f32[32]{0:T(128)S(1)} %iota_convert_fusion), kind=kOutput, calls=%fused_computation.58 | convolution fusion | flops 25362432 | bytes 336000 | tf_op jit(solution)/shard_map/jxy,jky->jxk/dot_general | solution.py:49
  99.3 1.3 %fusion.18 = f32[16,32,128]{2,1,0:T(8,128)S(1)} fusion(f32[16,32,32]{2,1,0:T(8,128)S(1)} %get-tuple-element.27, f32[16,128]{1,0:T(8,128)S(1)} %get-tuple-element.37, f32[32]{0:T(128)S(1)} %iota_convert_fusion), kind=kOutput, calls=%fused_computation.57 | convolution fusion | flops 25296896 | bytes 336000 | tf_op jit(solution)/shard_map/jxy,jky->jxk/dot_general | solution.py:49
  100.6 1.3 %fusion.5 = f32[16,128,32]{1,2,0:T(8,128)S(1)} fusion(f32[16,32,128]{2,1,0:T(8,128)S(1)} %fusion.20, f32[16,32,32]{2,1,0:T(8,128)S(1)} %get-tuple-element.26, f32[16,128]{1,0:T(8,128)S(1)} %get-tuple-element.37, f32[32]{0:T(128)S(1)} %iota_convert_fusion), kind=kOutput, calls=%fused_computation.25 | convolution fusion | flops 25362432 | bytes 598144 | tf_op jit(solution)/shard_map/jxy,jky->jxk/dot_general | solution.py:49
  102.0 2.4 %multiply_reduce_fusion = (f32[16,128]{1,0:T(8,128)S(1)}, f32[16,128]{1,0:T(8,128)S(1)}, f32[16,128]{1,0:T(8,128)S(1)}, f32[16,128]{1,0:T(8,128)S(1)}) fusion(f32[32]{0:T(128)S(1)} %iota_convert_fusion, f32[16,128]{1,0:T(8,128)S(1)} %get-tuple-element.36, f32[16,128,32]{1,2,0:T(8,128)S(1)} %fusion.5, f32[16,32,128]{2,1,0:T(8,128)S(1)} %fusion.18, ...), kind=kOutput, calls=%fused_computation.48 | convolution fusion | flops 26140672 | bytes 639104 | tf_op jit(solution)/shard_map/jxy,jky->jxk/dot_general | solution.py:49
  104.4 0.1 collective-permute-start
  104.5 1.5 %collective-permute-start.1 = (f32[2,4,1,128]{3,1,0,2:T(4,128)S(1)}, f32[2,4,1,128]{3,1,0,2:T(4,128)S(1)}, u32[]{:S(2)}, u32[]{:S(2)}) collective-permute-start(f32[2,4,1,128]{3,1,0,2:T(4,128)S(1)} %bitcast.114), channel_id=1, source_target_pairs={{0,4},{2,6},{4,0},{6,2},{1,5},{3,7},{5,1},{7,3},{8,12},{10,14},{12... | collective-permute-start | bytes 12296 | tf_op jit(solution)/shard_map/ppermute | solution.py:34
  106.0 0.3 collective-permute-start.2
  106.3 0.0 collective-permute-done
  106.3 1.8 %collective-permute-done.1 = f32[2,4,1,128]{3,1,0,2:T(4,128)S(1)} collective-permute-done((f32[2,4,1,128]{3,1,0,2:T(4,128)S(1)}, f32[2,4,1,128]{3,1,0,2:T(4,128)S(1)}, u32[]{:S(2)}, u32[]{:S(2)}) %collective-permute-start.1) | collective-permute-done | bytes 4128 | tf_op jit(solution)/shard_map/ppermute | solution.py:34
  108.2 0.9 collective-permute-done.2
  109.0 0.6 gather_fusion.2
  109.6 0.0 copy-done.1
  109.6 0.6 broadcast_select_fusion
  (16 shorter events, 0.1 us)
Async XLA Ops:
  6.5 2.6 %copy-start = (f32[2,64,1024]{2,1,0:T(8,128)S(1)}, f32[2,64,1024]{2,1,0:T(8,128)}, u32[]{:S(2)}) copy-start(f32[2,64,1024]{2,1,0:T(8,128)} %param.8) | copy-start | bytes 1572868
  6.5 46.8 %all-gather.2.cloned.1.call-start = ((), (), s32[]{:S(2)}) async-start(), calls=%async_computation.1 | async-start | bytes 1310720 | tf_op jit(solution)/shard_map/all_gather | solution.py:160
  7.3 84.6 %reduce-scatter.2.cloned.1.call-start = ((), (), s32[]{:S(2)}) async-start(), calls=%async_computation.2 | async-start | bytes 393216 | tf_op jit(solution)/shard_map/reduce_scatter | solution.py:167
  67.4 9.9 %copy-start.2 = (f32[2,16,128]{2,1,0:T(8,128)S(1)}, f32[2,16,128]{2,1,0:T(8,128)}, u32[]{:S(2)}) copy-start(f32[2,16,128]{2,1,0:T(8,128)} %param.11) | copy-start | bytes 49156
  75.8 33.9 %copy-start.1 = (f32[2,4,1,512]{3,2,1,0:T(1,128)S(1)}, f32[2,4,1,512]{3,2,1,0:T(1,128)}, u32[]{:S(2)}) copy-start(f32[2,4,1,512]{3,2,1,0:T(1,128)} %param.12) | copy-start | bytes 49156
  104.4 1.9 %collective-permute-start = (f32[2,4,1,128]{3,1,0,2:T(4,128)S(1)}, f32[2,4,1,128]{3,1,0,2:T(4,128)S(1)}, u32[]{:S(2)}, u32[]{:S(2)}) collective-permute-start(f32[2,4,1,128]{3,1,0,2:T(4,128)S(1)} %bitcast.115), channel_id=1, source_target_pairs={{0,2},{2,0},{4,6},{6,4},{1,3},{3,1},{5,7},{7,5},{8,10},{10,8},{12,... | collective-permute-start | bytes 12296 | tf_op jit(solution)/shard_map/ppermute | solution.py:34
  104.5 3.7 %collective-permute-start.1 = (f32[2,4,1,128]{3,1,0,2:T(4,128)S(1)}, f32[2,4,1,128]{3,1,0,2:T(4,128)S(1)}, u32[]{:S(2)}, u32[]{:S(2)}) collective-permute-start(f32[2,4,1,128]{3,1,0,2:T(4,128)S(1)} %bitcast.114), channel_id=1, source_target_pairs={{0,4},{2,6},{4,0},{6,2},{1,5},{3,7},{5,1},{7,3},{8,12},{10,14},{12... | collective-permute-start | bytes 12296 | tf_op jit(solution)/shard_map/ppermute | solution.py:34
  106.0 3.0 %collective-permute-start.2 = (f32[2,4,1,128]{3,1,0,2:T(4,128)S(1)}, f32[2,4,1,128]{3,1,0,2:T(4,128)S(1)}, u32[]{:S(2)}, u32[]{:S(2)}) collective-permute-start(f32[2,4,1,128]{3,1,0,2:T(4,128)S(1)} %bitcast.113), channel_id=1, source_target_pairs={{0,6},{2,4},{4,2},{6,0},{1,7},{3,5},{5,3},{7,1},{8,14},{10,12},{12... | collective-permute-start | bytes 12296 | tf_op jit(solution)/shard_map/ppermute | solution.py:34
Sparse Core Ops, SparseCore 0:
  8.9 30.8 all-gather.1
  77.3 14.4 reduce-scatter.1
